TPU v7x, 32 devices: a whole 2x2x4 slice. The times are simulated.
32 devices in a mesh: pipe: 8 (over z, y), tensor: 4 (over x, core).
Axes of the slice: x: 2, y: 2, z: 4, core: 2. Of those that a mesh axis runs over, the one named last changes fastest.
Arguments:
- memory: bfloat16 [2, 512, 4096], P(None, 'pipe', 'tensor'), may hold values from -6 to 6
- states: bfloat16 [8, 2, 256, 4096], P('pipe', None, None, 'tensor'), may hold values from -6 to 6
- norm_gain: float32 [8, 4096], P('pipe'), may hold values from 0.25 to 1.75
- w_query: bfloat16 [8, 4096, 4096], P('pipe', None, 'tensor'), may hold values from -0.09375 to 0.09375
- w_keyvalue: bfloat16 [8, 4096, 2, 4096], P('pipe', None, None, 'tensor'), may hold values from -0.09375 to 0.09375
- w_output: bfloat16 [8, 4096, 4096], P('pipe', 'tensor'), may hold values from -0.125 to 0.125
Outputs:
- updated: bfloat16 [8, 2, 256, 4096], P('pipe', None, None, 'tensor')
All inputs are finite; a program needn't handle non-finite values.
Results may differ from a plain program's by a relative error of at most 0.006.
Values may be sent and summed in bfloat16 or wider, within the bound.
A program may use at most 128 MiB of HBM per device.

v0:
```python
import jax
import jax.numpy as jnp
from jax import lax
from jax.sharding import PartitionSpec as P

HEAD_DIM = 64


def per_device(memory, states, norm_gain, w_query, w_keyvalue, w_output):
    whole_states = lax.all_gather(states[0], "tensor", axis=2, tiled=True)
    xf = whole_states.astype(jnp.float32)
    scale = lax.rsqrt(jnp.mean(xf * xf, axis=-1, keepdims=True) + 1e-06)
    normed = (xf * scale * norm_gain[0]).astype(jnp.bfloat16)
    weight_q = w_query[0]
    local_inner = weight_q.shape[1]
    weight_kv = w_keyvalue[0].reshape(w_keyvalue.shape[1], 2 * local_inner)
    weight_o = w_output[0]
    seqs = normed.shape[0]
    dec_rows = normed.shape[1]
    local_heads = local_inner // HEAD_DIM
    query = jnp.einsum("btd,de->bte", normed, weight_q, preferred_element_type=jnp.float32).astype(
        jnp.bfloat16
    )
    gathered = lax.all_gather(memory, "pipe", axis=1, tiled=True)
    gathered = lax.all_gather(gathered, "tensor", axis=2, tiled=True)
    keyvalue = jnp.einsum(
        "bpd,de->bpe", gathered, weight_kv, preferred_element_type=jnp.float32
    ).astype(jnp.bfloat16)
    enc_rows = keyvalue.shape[1]
    keys = keyvalue[:, :, :local_inner].reshape(seqs, enc_rows, local_heads, HEAD_DIM)
    values = keyvalue[:, :, local_inner:].reshape(seqs, enc_rows, local_heads, HEAD_DIM)
    heads_q = query.reshape(seqs, dec_rows, local_heads, HEAD_DIM)
    scores = jnp.einsum(
        "bqhd,bkhd->bhqk", heads_q, keys, preferred_element_type=jnp.float32
    ) / jnp.sqrt(jnp.float32(HEAD_DIM))
    probs = jax.nn.softmax(scores, axis=-1).astype(jnp.bfloat16)
    context = jnp.einsum(
        "bhqk,bkhd->bqhd", probs, values, preferred_element_type=jnp.float32
    ).astype(jnp.bfloat16)
    context = context.reshape(seqs, dec_rows, local_inner)
    partial_terms = jnp.einsum("bte,ed->btd", context, weight_o, preferred_element_type=jnp.float32)
    branch = lax.psum_scatter(partial_terms, "tensor", scatter_dimension=2, tiled=True)
    result = (states[0].astype(jnp.float32) + branch).astype(jnp.bfloat16)
    return result[None]


def solution(mesh):
    in_specs = (
        P(None, "pipe", "tensor"),
        P("pipe", None, None, "tensor"),
        P("pipe", None),
        P("pipe", None, "tensor"),
        P("pipe", None, None, "tensor"),
        P("pipe", "tensor", None),
    )
    out_specs = P("pipe", None, None, "tensor")
    return jax.shard_map(
        per_device, mesh=mesh, in_specs=in_specs, out_specs=out_specs, check_vma=False
    )
```

profile of v0, /device:TPU:8, one launch (start us, length us, event | category | flops | bytes accessed | tf_op | source)
XLA Modules:
  0.0 293.3 jit_solution(15955444793238928033)
XLA Ops:
  6.5 0.0 all-gather.5.cloned.1.call-start
  6.5 0.7 all-gather.5.cloned.1.call-update
  7.3 0.0 all-gather.9.cloned.1.call-start
  7.3 0.7 all-gather.9.cloned.1.call-update
  8.0 0.0 all-gather.7.cloned.1.call-start
  8.1 51.8 %all-gather.5.cloned.1.call-done = bf16[2,512,1024]{2,1,0:T(8,128)(2,1)} async-done(((bf16[2,64,1024]{2,1,0:T(8,128)(2,1)}), bf16[2,512,1024]{2,1,0:T(8,128)(2,1)}) %all-gather.5.cloned.1.call-update) | async-done | bytes 2097168 | tf_op jit(solution)/shard_map/all_gather | solution.py:24
  59.8 0.0 all-gather.7.cloned.1.call-update
  59.8 0.0 copy-start.2
  59.9 0.0 reduce-scatter.2.cloned.1.call-start
  59.9 27.9 %reshape.30 = bf16[4096,2048,1]{1,0,2:T(8,128)(2,1)} reshape(bf16[1,4096,2,1024]{3,2,1,0:T(2,128)(2,1)} %param.10) | data formatting | bytes 33554432 | tf_op jit(solution)/shard_map/reshape;squeeze | solution.py:16
  87.8 6.5 %all-gather.9.cloned.1.call-done = bf16[1,2,256,4096]{3,2,1,0:T(8,128)(2,1)} async-done(((bf16[1,2,256,1024]{3,2,1,0:T(8,128)(2,1)}), bf16[1,2,256,4096]{3,2,1,0:T(8,128)(2,1)}) %all-gather.9.cloned.1.call-update) | async-done | bytes 4194320 | tf_op jit(solution)/shard_map/all_gather | solution.py:10
  94.4 3.1 %fusion.4 = f32[2,256]{1,0:T(2,128)S(1)} fusion(bf16[1,2,256,4096]{3,2,1,0:T(8,128)(2,1)} %all-gather.9.cloned.1.call-done), kind=kLoop, calls=%fused_computation.7 | loop fusion | flops 6290944 | bytes 4196352 | tf_op jit(solution)/shard_map/reduce_sum | solution.py:12
  97.4 0.0 copy-done.2
  97.5 9.2 %fusion.21 = bf16[2,256,1024]{2,1,0:T(8,128)(2,1)S(1)} fusion(bf16[1,4096,1024]{2,1,0:T(8,128)(2,1)} %param.9, bf16[1,2,256,4096]{3,2,1,0:T(8,128)(2,1)} %all-gather.9.cloned.1.call-done, f32[4096]{0:T(1024)S(1)} %bitcast.43, f32[2,256]{1,0:T(2,128)S(1)} %add_rsqrt_fusion), kind=kOutput, calls=%fused_computation.24 | convolution fusion | flops 4303880192 | bytes 13649920 | tf_op jit(solution)/shard_map/btd,de->bte/dot_general | solution.py:21
  106.7 0.5 copy.12
  107.2 47.0 %all-gather.7.cloned.1.call-done = bf16[2,512,4096]{2,1,0:T(8,128)(2,1)} async-done(((bf16[2,512,1024]{2,1,0:T(8,128)(2,1)}), bf16[2,512,4096]{2,1,0:T(8,128)(2,1)}) %all-gather.7.cloned.1.call-update) | async-done | bytes 8388624 | tf_op jit(solution)/shard_map/all_gather | solution.py:25
  154.2 22.7 %convolution_convert_fusion = bf16[2,512,2048]{2,1,0:T(8,128)(2,1)S(1)} fusion(bf16[2,512,4096]{2,1,0:T(8,128)(2,1)} %all-gather.7.cloned.1.call-done, bf16[4096,2048,1]{1,0,2:T(8,128)(2,1)} %reshape.30), kind=kOutput, calls=%fused_computation.19 | convolution fusion | flops 17181966336 | bytes 29360128 | tf_op jit(solution)/shard_map/bpd,de->bpe/dot_general | solution.py:26
  176.9 1.8 fusion.28
  178.7 3.9 %copy.11 = bf16[2,512,1024]{1,2,0:T(8,128)(2,1)} copy(bf16[2,512,1024]{2,1,0:T(8,128)(2,1)} %get-tuple-element.6) | data formatting | bytes 4194304 | tf_op jit(solution)/shard_map/slice | solution.py:31
  182.6 2.5 copy.13
  185.2 0.0 copy-start.1
  185.2 9.8 %fusion.29 = (f32[2,16,256]{2,1,0:T(8,128)S(1)}, f32[2,16,256,512]{3,2,1,0:T(8,128)}) fusion(bf16[2,256,16,64]{1,3,2,0:T(8,128)(2,1)S(1)} %bitcast.42, bf16[2,512,16,64]{1,3,2,0:T(8,128)(2,1)} %bitcast.40), kind=kOutput, calls=%fused_computation.29 | convolution fusion | flops 549454336 | bytes 19955712 | tf_op jit(solution)/shard_map/sub | solution.py:36
  194.9 0.0 copy-done.1
  194.9 7.3 %fusion.20 = bf16[2,16,64,256]{3,2,1,0:T(8,128)(2,1)S(1)} fusion(bf16[2,512,16,64]{1,3,2,0:T(8,128)(2,1)S(1)} %bitcast.39, f32[2,16,256,512]{3,2,1,0:T(8,128)} %get-tuple-element.8, f32[2,16,256]{2,1,0:T(8,128)S(1)} %get-tuple-element.7), kind=kOutput, calls=%fused_computation.23 | convolution fusion | flops 545783808 | bytes 19955712 | tf_op jit(solution)/shard_map/bhqk,bkhd->bqhd/dot_general | solution.py:37
  202.2 10.2 %fusion.7 = f32[2,256,4096]{2,1,0:T(8,128)} fusion(bf16[2,256,1024]{1,2,0:T(8,128)(2,1)S(1)} %bitcast.41, bf16[1,1024,4096]{2,1,0:T(8,128)(2,1)} %param.11), kind=kOutput, calls=%fused_computation.10 | convolution fusion | flops 4294967296 | bytes 17825792 | tf_op jit(solution)/shard_map/bte,ed->btd/dot_general | solution.py:41
  212.4 0.0 copy-start
  212.4 0.0 reduce-scatter.2.cloned.1.call-update
  212.4 71.4 %reduce-scatter.2.cloned.1.call-done = f32[2,256,1024]{2,1,0:T(8,128)} async-done(((f32[2,256,4096]{2,1,0:T(8,128)}), f32[2,256,1024]{2,1,0:T(8,128)}) %reduce-scatter.2.cloned.1.call-update) | async-done | bytes 2097168 | tf_op jit(solution)/shard_map/reduce_scatter | solution.py:42
  283.8 0.0 copy-done
  283.8 2.9 fusion.26
  (1 shorter events, 0.0 us)
Async XLA Ops:
  6.5 53.3 %all-gather.5.cloned.1.call-start = ((), (), s32[]{:S(2)}) async-start(), calls=%async_computation.1 | async-start | bytes 2359296 | tf_op jit(solution)/shard_map/all_gather | solution.py:24
  7.3 87.1 %all-gather.9.cloned.1.call-start = ((), (), s32[]{:S(2)}) async-start(), calls=%async_computation.4 | async-start | bytes 5242880 | tf_op jit(solution)/shard_map/all_gather | solution.py:10
  8.0 146.2 %all-gather.7.cloned.1.call-start = ((), (), s32[]{:S(2)}) async-start(), calls=%async_computation.2 | async-start | bytes 10485760 | tf_op jit(solution)/shard_map/all_gather | solution.py:25
  59.8 37.6 %copy-start.2 = (f32[1,4096]{1,0:T(1,128)S(1)}, f32[1,4096]{1,0:T(1,128)}, u32[]{:S(2)}) copy-start(f32[1,4096]{1,0:T(1,128)} %param.8) | copy-start | bytes 49156
  59.9 224.0 %reduce-scatter.2.cloned.1.call-start = ((), (), s32[]{:S(2)}) async-start(), calls=%async_computation.3 | async-start | bytes 10485760 | tf_op jit(solution)/shard_map/reduce_scatter | solution.py:42
  185.2 9.8 %copy-start.1 = (bf16[2,512,1024]{1,2,0:T(8,128)(2,1)S(1)}, bf16[2,512,1024]{1,2,0:T(8,128)(2,1)}, u32[]{:S(2)}) copy-start(bf16[2,512,1024]{1,2,0:T(8,128)(2,1)} %copy.11) | copy-start | bytes 6291460
  212.4 71.4 %copy-start = (bf16[1,2,256,1024]{3,2,1,0:T(8,128)(2,1)S(1)}, bf16[1,2,256,1024]{3,2,1,0:T(8,128)(2,1)}, u32[]{:S(2)}) copy-start(bf16[1,2,256,1024]{3,2,1,0:T(8,128)(2,1)} %param.7) | copy-start | bytes 3145732
Sparse Core Ops, SparseCore 0:
  9.5 50.2 all-gather.4
  61.4 32.9 all-gather.8
  95.9 58.2 all-gather.6
  212.5 71.2 reduce-scatter.1
where the time goes:
time: 296 us; the launch traced here: 293 us
  waiting for transfers between devices  178 us (60%)
  matrix products  59.1 us (20%)
  local copies, waits for them, and re-layouts  36.7 us (12%)
  between operations  13.2 us (4%)
  other arithmetic  6 us (2%)
    reduce_scatter x1, waiting for transfers between devices, per_device(): lax.psum_scatter(partial_terms, 'tensor', scatter_dimension=2, tiled=True)  71.4 us
    all_gather x1, waiting for transfers between devices, per_device(): gathered = lax.all_gather(memory, 'pipe', axis=1, tiled=True)  51.8 us
    all_gather x1, waiting for transfers between devices, per_device(): gathered = lax.all_gather(gathered, 'tensor', axis=2, tiled=True)  47 us
    another operation x1, local copies, waits for them, and re-layouts, per_device(): weight_kv = w_keyvalue[0].reshape(w_keyvalue.shape[1], 2 * local_inner)  27.9 us
    dot_general x1, matrix products, per_device(): jnp.einsum('bpd,de->bpe', gathered, weight_kv, preferred_element_type=jnp...  22.7 us
    dot_general x1, matrix products, per_device(): jnp.einsum('bte,ed->btd', context, weight_o, preferred_element_type=jnp.f...  10.2 us
    sub x1, matrix products, per_device(): probs = jax.nn.softmax(scores, axis=-1).astype(jnp.bfloat16)  9.75 us
    dot_general x1, matrix products, per_device(): jnp.einsum('btd,de->bte', normed, weight_q, preferred_element_type=jnp.fl...  9.2 us
  transfers between devices with their start and end apart: 4, of which 4 were waited for; matrix products, arithmetic and copies ran while one was open for 14% of the time, Pallas kernels for 0%

commit v1 on v0

--- a/solution.py
+++ b/solution.py
@@ -1,9 +1,393 @@
+import functools
+
 import jax
 import jax.numpy as jnp
 from jax import lax
+from jax.experimental import pallas as pl
+from jax.experimental.pallas import tpu as pltpu
 from jax.sharding import PartitionSpec as P
 
 HEAD_DIM = 64
+CORES = 2
+LOW = 2
+TILE = 256
+MAX_COPIES = 100
+MESH = pl.DeviceIdType.MESH
+F32 = jnp.float32
+BF16 = jnp.bfloat16
+
+
+def copies_per_sequence(n_pipe, n_tensor):
+    xs, highs = n_tensor // CORES, n_pipe // LOW
+    return 4 * n_pipe * xs + (xs - 1) * highs
+
+
+def kernel(
+    n_pipe, n_tensor,
+    mem_hbm, st_hbm, gain_ref, wq_hbm, wkv_hbm, wo_hbm, out_ref,
+    mem, st, wq, wkv, wo, q, kv, ctx, pd, rd, px, rx, part,
+    load_sem, send_sem, recv_ici, recv_d2d, st_ici, st_d2d, pd_sem, px_sem,
+):
+    xs, highs = n_tensor // CORES, n_pipe // LOW
+    seqs, enc, depth = mem.shape
+    rows = st.shape[1]
+    pos = enc // n_pipe
+    feat = depth // n_tensor
+    inner = wq.shape[1]
+    pipe = lax.axis_index("pipe")
+    tensor = lax.axis_index("tensor")
+    hi, lo = pipe // LOW, pipe % LOW
+    x, core = tensor // CORES, tensor % CORES
+    other_lo, other_core = 1 - lo, 1 - core
+
+    def turn(a, k, n):
+        return lax.rem(a + k, n)
+
+    def device(h, l, xx, c):
+        return (h * LOW + l, xx * CORES + c)
+
+    x_peers = [device(hi, lo, turn(x, j, xs), core) for j in range(1, xs)]
+    hi_peers = [device(turn(hi, k, highs), lo, x, core) for k in range(1, highs)]
+    lo_peer = device(hi, other_lo, x, core)
+    sibling = device(hi, lo, x, other_core)
+
+    def block(s, p, xx, c):
+        r = pl.multiple_of(p * pos, pos)
+        f = pl.multiple_of((xx * CORES + c) * feat, feat)
+        return mem.at[s, pl.ds(r, pos), pl.ds(f, feat)]
+
+    def st_block(s, xx, c):
+        return st.at[s, :, pl.ds(pl.multiple_of((xx * CORES + c) * feat, feat), feat)]
+
+    sends = []
+    counter = [0]
+
+    def new_sems(n=1):
+        first = counter[0]
+        counter[0] += n
+        return first
+
+    def remote(src, dst, sem, recv, dev):
+        return pltpu.make_async_remote_copy(
+            src_ref=src, dst_ref=dst, send_sem=send_sem.at[sem], recv_sem=recv,
+            device_id=dev, device_id_type=MESH,
+        )
+
+    def send(src, dst, recv, dev):
+        copy = remote(src, dst, new_sems(), recv, dev)
+        copy.start()
+        sends.append(copy)
+        return copy
+
+    st_sends = [[], []]
+
+    def send_states(s, ref, recv, dev):
+        st_sends[s].append(send(ref, ref, recv, dev))
+        sends.pop()
+
+    def send_block(s, p, xx, dev, recv):
+        ref = block(s, p, xx, core)
+        send(ref, ref, recv.at[s, p * xs + xx], dev)
+
+    def wait_block(s, p, xx):
+        ref = block(s, p, xx, core)
+        remote(ref, ref, 0, recv_ici.at[s, p * xs + xx], sibling).wait_recv()
+
+    loads = [
+        pltpu.make_async_copy(mem_hbm.at[0], block(0, pipe, x, core), load_sem.at[0]),
+        pltpu.make_async_copy(st_hbm.at[0], st_block(0, x, core), load_sem.at[1]),
+        pltpu.make_async_copy(mem_hbm.at[1], block(1, pipe, x, core), load_sem.at[2]),
+        pltpu.make_async_copy(st_hbm.at[1], st_block(1, x, core), load_sem.at[3]),
+    ]
+    weights = [
+        pltpu.make_async_copy(wkv_hbm, wkv, load_sem.at[4]),
+        pltpu.make_async_copy(wq_hbm, wq, load_sem.at[5]),
+        pltpu.make_async_copy(wo_hbm, wo, load_sem.at[6]),
+    ]
+    for copy in loads:
+        copy.start()
+    barrier = pltpu.get_barrier_semaphore()
+    peers = x_peers + hi_peers + [lo_peer, sibling]
+    for peer in peers:
+        pl.semaphore_signal(barrier, inc=1, device_id=peer, device_id_type=MESH)
+    pl.semaphore_wait(barrier, len(peers))
+
+    def first_sends(s):
+        loads[2 * s].wait()
+        for dev in x_peers:
+            send_block(s, pipe, x, dev, recv_ici)
+        send_block(s, pipe, x, lo_peer, recv_ici)
+        for dev in hi_peers:
+            send_block(s, pipe, x, dev, recv_ici)
+        send_block(s, pipe, x, sibling, recv_d2d)
+
+    def state_sends(s):
+        loads[2 * s + 1].wait()
+        ref = st_block(s, x, core)
+        for dev in x_peers:
+            send_states(s, ref, st_ici.at[s, x], dev)
+        send_states(s, ref, st_d2d.at[s, x], sibling)
+
+    def forward_x(s):
+        for j in range(1, xs):
+            xx = turn(x, j, xs)
+            wait_block(s, pipe, xx)
+            send_block(s, pipe, xx, lo_peer, recv_ici)
+            for dev in hi_peers:
+                send_block(s, pipe, xx, dev, recv_ici)
+            send_block(s, pipe, xx, sibling, recv_d2d)
+
+    n_high = (highs - 1) * xs
+
+    def high_copies(s, i, base):
+        k, j = 1 + i // xs, i % xs
+        p, xx = turn(hi, k, highs) * LOW + lo, turn(x, j, xs)
+        ref = block(s, p, xx, core)
+        slot = p * xs + xx
+        arrived = remote(ref, ref, 0, recv_ici.at[s, slot], sibling)
+        return (
+            arrived,
+            remote(ref, ref, base + 2 * i, recv_ici.at[s, slot], lo_peer),
+            remote(ref, ref, base + 2 * i + 1, recv_d2d.at[s, slot], sibling),
+        )
+
+    def forward_high(s, i, base):
+        arrived, over_low, over = high_copies(s, i, base)
+        arrived.wait_recv()
+        over_low.start()
+        over.start()
+
+    high_base = [new_sems(2 * n_high), new_sems(2 * n_high)]
+
+    def forward_low(s):
+        for k in range(highs):
+            for j in range(xs):
+                p, xx = turn(hi, k, highs) * LOW + other_lo, turn(x, j, xs)
+                wait_block(s, p, xx)
+                send_block(s, p, xx, sibling, recv_d2d)
+
+    def forward_states(s):
+        for j in range(1, xs):
+            xx = turn(x, j, xs)
+            ref = st_block(s, xx, core)
+            remote(ref, ref, 0, st_ici.at[s, xx], sibling).wait_recv()
+            send_states(s, ref, st_d2d.at[s, xx], sibling)
+
+    def finish_states(s):
+        for xx in range(xs):
+            ref = st_block(s, xx, other_core)
+            remote(ref, ref, 0, st_d2d.at[s, xx], sibling).wait_recv()
+
+    def finish_memory(s):
+        for p in range(n_pipe):
+            for xx in range(xs):
+                ref = block(s, p, xx, other_core)
+                remote(ref, ref, 0, recv_d2d.at[s, p * xs + xx], sibling).wait_recv()
+
+    def query(s):
+        for copy in st_sends[s]:
+            copy.wait_send()
+        part[s] = st[s, :, pl.ds(pl.multiple_of(tensor * feat, feat), feat)].astype(F32)
+
+        @pl.loop(0, rows // 16)
+        def _(i):
+            some = pl.ds(pl.multiple_of(i * 16, 16), 16)
+            xf = st[s, some, :].astype(F32)
+            mean = jnp.sum(xf * xf, axis=-1, keepdims=True) * (1.0 / depth)
+            scale = lax.rsqrt(mean + 1e-06)
+            st[s, some, :] = (xf * scale * gain_ref[...]).astype(BF16)
+
+        if s == 0:
+            weights[1].wait()
+
+        @pl.loop(0, inner // TILE)
+        def _(i):
+            cols = pl.ds(pl.multiple_of(i * TILE, TILE), TILE)
+            full = jnp.dot(st[s], wq[:, cols], preferred_element_type=F32)
+            q[s, :, cols] = full.astype(BF16) * jnp.array(HEAD_DIM ** -0.5, BF16)
+
+    def kv_tile(s, i):
+        cols = pl.ds(pl.multiple_of(i * TILE, TILE), TILE)
+        full = jnp.dot(mem[s], wkv[:, cols], preferred_element_type=F32)
+        kv[:, cols] = full.astype(BF16)
+
+    def attention(s):
+        lane = lax.broadcasted_iota(jnp.int32, (1, 2 * HEAD_DIM), 1)
+        first = lane < HEAD_DIM
+
+        @pl.loop(0, inner // (2 * HEAD_DIM))
+        def _(i):
+            cols = pl.ds(pl.multiple_of(i * 2 * HEAD_DIM, 2 * HEAD_DIM), 2 * HEAD_DIM)
+            vcols = pl.ds(pl.multiple_of(inner + i * 2 * HEAD_DIM, 2 * HEAD_DIM), 2 * HEAD_DIM)
+            qp, kp, vp = q[s, :, cols], kv[:, cols], kv[:, vcols]
+            outs = []
+            for mine in (first, jnp.logical_not(first)):
+                qh = jnp.where(mine, qp, jnp.zeros_like(qp))
+                vh = jnp.where(mine, vp, jnp.ones_like(vp))
+                scores = lax.dot_general(
+                    qh, kp, (((1,), (1,)), ((), ())), preferred_element_type=F32
+                )
+                top = jnp.max(scores, axis=-1, keepdims=True)
+                probs = jnp.exp(scores - top).astype(BF16)
+                outs.append(jnp.dot(probs, vh, preferred_element_type=F32))
+            total = jnp.where(first, outs[0], outs[1])
+            sums = pltpu.roll(jnp.where(first, outs[1], outs[0]), HEAD_DIM, 1)
+            ctx[:, cols] = (total / sums).astype(BF16)
+
+    width = min(TILE, feat)
+
+    def product(t, i):
+        cols = pl.ds(pl.multiple_of(t * feat + i * width, width), width)
+        return jnp.dot(ctx[...], wo[:, cols], preferred_element_type=F32)
+
+    def tile(i):
+        return pl.ds(pl.multiple_of(i * width, width), width)
+
+    def output(s):
+        if s == 0:
+            weights[2].wait()
+        steps = feat // width
+        order = [turn(x, j, xs) for j in range(1, xs)] + [x]
+        for j, xx in enumerate(order):
+            @pl.loop(0, steps)
+            def _(i):
+                pd[s, j, :, tile(i)] = product(xx * CORES + other_core, i).astype(BF16)
+
+            send(pd.at[s, j], rd.at[s, j], pd_sem.at[s, j], sibling)
+            if j < xs - 1:
+                @pl.loop(0, steps)
+                def _(i):
+                    px[s, j, :, tile(i)] = product(xx * CORES + core, i).astype(BF16)
+
+                remote(pd.at[s, j], rd.at[s, j], 0, pd_sem.at[s, j], sibling).wait_recv()
+                px[s, j] = (px[s, j].astype(F32) + rd[s, j].astype(F32)).astype(BF16)
+                send(px.at[s, j], rx.at[s, j], px_sem.at[s, j], x_peers[j])
+
+    def result(s):
+        j = xs - 1
+        remote(pd.at[s, j], rd.at[s, j], 0, pd_sem.at[s, j], sibling).wait_recv()
+
+        @pl.loop(0, feat // width)
+        def _(i):
+            c = tile(i)
+            part[s, :, c] += product(tensor, i) + rd[s, j, :, c].astype(F32)
+
+    def finish(s):
+        for j in range(xs - 1):
+            remote(px.at[s, j], rx.at[s, j], 0, px_sem.at[s, j], sibling).wait_recv()
+
+        @pl.loop(0, feat // width)
+        def _(i):
+            c = tile(i)
+            total = part[s, :, c]
+            for j in range(xs - 1):
+                total += rx[s, j, :, c].astype(F32)
+            out_ref[s, :, c] = total.astype(BF16)
+
+    for s in range(seqs):
+        first_sends(s)
+        state_sends(s)
+        if s == 0:
+            for copy in weights:
+                copy.start()
+    forward_x(0)
+    half = n_high // 2
+    for i in range(half):
+        forward_high(0, i, high_base[0])
+    forward_x(1)
+    for i in range(half, n_high):
+        forward_high(0, i, high_base[0])
+    forward_states(0)
+    finish_states(0)
+    query(0)
+    forward_low(0)
+    weights[0].wait()
+    finish_memory(0)
+    tiles = 2 * inner // TILE
+
+    @pl.loop(0, tiles)
+    def _(i):
+        @pl.when(i < n_high)
+        def _():
+            forward_high(1, i, high_base[1])
+
+        kv_tile(0, i)
+
+    for i in range(tiles, n_high):
+        forward_high(1, i, high_base[1])
+    attention(0)
+    output(0)
+    result(0)
+    forward_states(1)
+    finish_states(1)
+    query(1)
+    forward_low(1)
+    finish_memory(1)
+
+    @pl.loop(0, tiles)
+    def _(i):
+        kv_tile(1, i)
+
+    attention(1)
+    output(1)
+    result(1)
+    finish(0)
+    finish(1)
+    for copy in sends:
+        copy.wait_send()
+    for s in range(seqs):
+        for i in range(n_high):
+            arrived, over_low, over = high_copies(s, i, high_base[s])
+            over_low.wait_send()
+            over.wait_send()
+
+
+def fused(n_pipe, n_tensor, memory, states, norm_gain, w_query, w_keyvalue, w_output):
+    seqs, pos, feat = memory.shape
+    rows = states.shape[2]
+    depth, inner = feat * n_tensor, w_query.shape[2]
+    enc = pos * n_pipe
+    xs, highs = n_tensor // CORES, n_pipe // LOW
+    weight_kv = w_keyvalue[0].reshape(depth, 2 * inner)
+    blocks = n_pipe * xs
+    per_seq = ((xs - 1) + (highs - 1) + 2 + (xs - 1) * (highs + 1) + 2 * (highs - 1) * xs
+               + highs * xs + 2 * xs + 2 * xs)
+    any_space = pl.BlockSpec(memory_space=pl.ANY)
+    in_vmem = pl.BlockSpec(memory_space=pltpu.VMEM)
+    dma = pltpu.SemaphoreType.DMA
+    out = pl.pallas_call(
+        functools.partial(kernel, n_pipe, n_tensor),
+        out_shape=jax.ShapeDtypeStruct((seqs, rows, feat), BF16),
+        in_specs=[any_space, any_space, in_vmem, any_space, any_space, any_space],
+        out_specs=in_vmem,
+        scratch_shapes=[
+            pltpu.VMEM((seqs, enc, depth), BF16),
+            pltpu.VMEM((seqs, rows, depth), BF16),
+            pltpu.VMEM((depth, inner), BF16),
+            pltpu.VMEM((depth, 2 * inner), BF16),
+            pltpu.VMEM((inner, depth), BF16),
+            pltpu.VMEM((seqs, rows, inner), BF16),
+            pltpu.VMEM((enc, 2 * inner), BF16),
+            pltpu.VMEM((rows, inner), BF16),
+            pltpu.VMEM((seqs, xs, rows, feat), BF16),
+            pltpu.VMEM((seqs, xs, rows, feat), BF16),
+            pltpu.VMEM((seqs, xs - 1, rows, feat), BF16),
+            pltpu.VMEM((seqs, xs - 1, rows, feat), BF16),
+            pltpu.VMEM((seqs, rows, feat), F32),
+            dma((7,)),
+            dma((seqs * per_seq,)),
+            dma((seqs, blocks)),
+            dma((seqs, blocks)),
+            dma((seqs, xs)),
+            dma((seqs, xs)),
+            dma((seqs, xs)),
+            dma((seqs, xs - 1)),
+        ],
+        compiler_params=pltpu.CompilerParams(
+            collective_id=0, has_side_effects=True, vmem_limit_bytes=66_000_000
+        ),
+    )(memory, states[0], norm_gain, w_query[0], weight_kv, w_output[0])
+    return out[None]
 
 
 def per_device(memory, states, norm_gain, w_query, w_keyvalue, w_output):
@@ -54,6 +438,11 @@
         P("pipe", "tensor", None),
     )
     out_specs = P("pipe", None, None, "tensor")
+    n_pipe, n_tensor = mesh.shape["pipe"], mesh.shape["tensor"]
+    even = n_pipe % LOW == 0 and n_tensor % CORES == 0 and n_pipe > LOW and n_tensor > CORES
+    body = per_device
+    if even and copies_per_sequence(n_pipe, n_tensor) <= MAX_COPIES:
+        body = functools.partial(fused, n_pipe, n_tensor)
     return jax.shard_map(
-        per_device, mesh=mesh, in_specs=in_specs, out_specs=out_specs, check_vma=False
+        body, mesh=mesh, in_specs=in_specs, out_specs=out_specs, check_vma=False
     )

time: 296 us -> 153 us (0.52)
  waiting for transfers between devices: 178 us -> 0 us
  Pallas kernels: 0 us -> 134 us
  matrix products: 59.1 us -> 0 us
  local copies, waits for them, and re-layouts: 36.7 us -> 19.4 us
  between operations: 13.2 us -> 0.01 us
  other arithmetic: 6 us -> 0 us
    pallas_call x0 -> x1, Pallas kernels: none -> 134 us  [fused(): pl.pallas_call(functools.partial(kernel, n_pipe, n_tensor), out_shape=jax...]
    all_gather x3 -> x0, waiting for transfers between devices: 105 us -> none  [the longest x1 51.8 us: per_device(): gathered = lax.all_gather(memory, 'pipe', axis=1, tiled=True)]
    reduce_scatter x1 -> x0, waiting for transfers between devices: 71.4 us -> none  [per_device(): lax.psum_scatter(partial_terms, 'tensor', scatter_dimension=2, tiled=True)]
    dot_general x4 -> x0, matrix products: 49.3 us -> none  [the longest x1 22.7 us: per_device(): jnp.einsum('bpd,de->bpe', gathered, weight_kv, preferred_element_type=jnp...]
    another operation x1 -> x0, local copies, waits for them, and re-layouts: 27.9 us -> none  [per_device(): weight_kv = w_keyvalue[0].reshape(w_keyvalue.shape[1], 2 * local_inner)]
    unnamed x6 -> x2, local copies, waits for them, and re-layouts: 0.01 us -> 19.4 us
    sub x1 -> x0, matrix products: 9.75 us -> none  [per_device(): probs = jax.nn.softmax(scores, axis=-1).astype(jnp.bfloat16)]
    slice x3 -> x0, local copies, waits for them, and re-layouts: 8.24 us -> none  [the longest x2 4.31 us: per_device(): keyvalue[:, :, :local_inner].reshape(seqs, enc_rows, local_heads, HEAD_DIM)]
  transfers between devices with their start and end apart: 4 -> 0, of which waited for: 4 -> 0; matrix products, arithmetic and copies ran while one was open for 14% -> 0% of each run, Pallas kernels for 0% -> 0%
where the time goes in v1:
time: 153 us
  Pallas kernels  134 us (88%)
  local copies, waits for them, and re-layouts  19.4 us (13%)
    pallas_call x1, Pallas kernels, fused(): pl.pallas_call(functools.partial(kernel, n_pipe, n_tensor), out_shape=jax...  134 us
    unnamed x2, local copies, waits for them, and re-layouts  19.4 us

profile of v1, /device:TPU:8, one launch (start us, length us, event | category | flops | bytes accessed | tf_op | source)
XLA Modules:
  0.0 153.1 jit_solution(2665863463474712102)
XLA Ops:
  0.0 17.1 %copy.7 = bf16[512,8,2,1024]{3,1,2,0:T(8,128)(2,1)} copy(bf16[512,8,2,1024]{3,2,1,0:T(2,128)(2,1)} %bitcast.8) | data formatting | bytes 33554432
  17.1 133.8 %shard_map.64 = bf16[2,256,1024]{2,1,0:T(8,128)(2,1)} custom-call(bf16[2,64,1024]{2,1,0:T(8,128)(2,1)} %mem_hbm.1, bf16[2,256,1024]{2,1,0:T(8,128)(2,1)} %bitcast.12, f32[1,4096]{1,0:T(1,128)} %gain_ref.1, bf16[4096,1024]{1,0:T(8,128)(2,1)} %bitcast.9, bf16[4096,2048]{1,0:T(8,128)(2,1)} %bitcast.7, bf16[1024,4096]{1,0:T(8,128)(2,1)} %bitcast.10), custom_call_target="tpu_custom_call" | custom-call | tf_op jit(solution)/shard_map/pallas_call | solution.py:358
  150.9 2.3 %copy.9 = bf16[1,2,256,1024]{3,2,1,0:T(8,128)(2,1)} copy(bf16[1,2,256,1024]{3,2,1,0:T(8,128)(2,1)} %bitcast.11) | data formatting | bytes 2097152

commit v2 on v1

--- a/solution.py
+++ b/solution.py
@@ -12,6 +12,9 @@
 LOW = 2
 TILE = 256
 MAX_COPIES = 100
+LANES = 128
+SUB = 16
+CHUNK = 256
 MESH = pl.DeviceIdType.MESH
 F32 = jnp.float32
 BF16 = jnp.bfloat16
@@ -25,8 +28,8 @@
 def kernel(
     n_pipe, n_tensor,
     mem_hbm, st_hbm, gain_ref, wq_hbm, wkv_hbm, wo_hbm, out_ref,
-    mem, st, wq, wkv, wo, q, kv, ctx, pd, rd, px, rx, part,
-    load_sem, send_sem, recv_ici, recv_d2d, st_ici, st_d2d, pd_sem, px_sem,
+    mem, st, wq, wkv, wo, q, kv, ctx, pd, rd, px, rx, part, staged,
+    load_sem, stage_sem, send_sem, recv_ici, recv_d2d, st_ici, st_d2d, pd_sem, px_sem,
 ):
     xs, highs = n_tensor // CORES, n_pipe // LOW
     seqs, enc, depth = mem.shape
@@ -100,9 +103,8 @@
         pltpu.make_async_copy(st_hbm.at[1], st_block(1, x, core), load_sem.at[3]),
     ]
     weights = [
-        pltpu.make_async_copy(wkv_hbm, wkv, load_sem.at[4]),
-        pltpu.make_async_copy(wq_hbm, wq, load_sem.at[5]),
-        pltpu.make_async_copy(wo_hbm, wo, load_sem.at[6]),
+        pltpu.make_async_copy(wq_hbm, wq, load_sem.at[4]),
+        pltpu.make_async_copy(wo_hbm, wo, load_sem.at[5]),
     ]
     for copy in loads:
         copy.start()
@@ -198,7 +200,7 @@
             st[s, some, :] = (xf * scale * gain_ref[...]).astype(BF16)
 
         if s == 0:
-            weights[1].wait()
+            weights[0].wait()
 
         @pl.loop(0, inner // TILE)
         def _(i):
@@ -245,7 +247,7 @@
 
     def output(s):
         if s == 0:
-            weights[2].wait()
+            weights[1].wait()
         steps = feat // width
         order = [turn(x, j, xs) for j in range(1, xs)] + [x]
         for j, xx in enumerate(order):
@@ -284,13 +286,54 @@
                 total += rx[s, j, :, c].astype(F32)
             out_ref[s, :, c] = total.astype(BF16)
 
+    groups = 2 * inner // LANES
+    size = CHUNK * groups
+    chunks = depth // CHUNK
+
+    def stage(i, slot):
+        src = wkv_hbm.at[pl.ds(pl.multiple_of(i * size, size), size), :]
+        return pltpu.make_async_copy(src, staged.at[slot], stage_sem.at[slot])
+
+    def spread(begin, end):
+        span = SUB * groups
+        a = lax.broadcasted_iota(jnp.int32, (span, span), 0)
+        b = lax.broadcasted_iota(jnp.int32, (span, span), 1)
+        swap = (b == lax.rem(a, SUB) * groups + a // SUB).astype(F32).astype(BF16)
+
+        @pl.loop(begin, end)
+        def _(i):
+            slot = lax.rem(i, 2)
+            stage(i, slot).wait()
+
+            @pl.loop(0, CHUNK // (2 * SUB))
+            def _(m):
+                r = pl.multiple_of(m * 2 * span, 2 * span)
+                both = jnp.concatenate(
+                    [staged[slot, pl.ds(r, span), :], staged[slot, pl.ds(r + span, span), :]], axis=1
+                )
+                moved = jnp.dot(swap, both, preferred_element_type=F32).astype(BF16)
+                d = pl.multiple_of(i * CHUNK + m * 2 * SUB, 2 * SUB)
+                for g in range(groups):
+                    col = (g % 2) * inner + (g // 2) * LANES
+                    piece = moved[g * SUB:(g + 1) * SUB]
+                    wkv[pl.ds(d, SUB), col:col + LANES] = piece[:, :LANES]
+                    wkv[pl.ds(d + SUB, SUB), col:col + LANES] = piece[:, LANES:]
+
+            @pl.when(i + 2 < chunks)
+            def _():
+                stage(i + 2, slot).start()
+
+    for i in range(2):
+        stage(i, i).start()
     for s in range(seqs):
         first_sends(s)
         state_sends(s)
         if s == 0:
             for copy in weights:
                 copy.start()
+    spread(0, chunks // 4)
     forward_x(0)
+    spread(chunks // 4, chunks)
     half = n_high // 2
     for i in range(half):
         forward_high(0, i, high_base[0])
@@ -301,7 +344,9 @@
     finish_states(0)
     query(0)
     forward_low(0)
-    weights[0].wait()
+    forward_states(1)
+    finish_states(1)
+    query(1)
     finish_memory(0)
     tiles = 2 * inner // TILE
 
@@ -317,11 +362,8 @@
         forward_high(1, i, high_base[1])
     attention(0)
     output(0)
+    forward_low(1)
     result(0)
-    forward_states(1)
-    finish_states(1)
-    query(1)
-    forward_low(1)
     finish_memory(1)
 
     @pl.loop(0, tiles)
@@ -348,7 +390,9 @@
     depth, inner = feat * n_tensor, w_query.shape[2]
     enc = pos * n_pipe
     xs, highs = n_tensor // CORES, n_pipe // LOW
-    weight_kv = w_keyvalue[0].reshape(depth, 2 * inner)
+    groups = 2 * inner // LANES
+    weight_kv = w_keyvalue[0].reshape(depth, 2, inner // LANES, LANES)
+    weight_kv = weight_kv.transpose(0, 2, 1, 3).reshape(depth * groups, LANES)
     blocks = n_pipe * xs
     per_seq = ((xs - 1) + (highs - 1) + 2 + (xs - 1) * (highs + 1) + 2 * (highs - 1) * xs
                + highs * xs + 2 * xs + 2 * xs)
@@ -374,7 +418,9 @@
             pltpu.VMEM((seqs, xs - 1, rows, feat), BF16),
             pltpu.VMEM((seqs, xs - 1, rows, feat), BF16),
             pltpu.VMEM((seqs, rows, feat), F32),
-            dma((7,)),
+            pltpu.VMEM((2, CHUNK * groups, LANES), BF16),
+            dma((6,)),
+            dma((2,)),
             dma((seqs * per_seq,)),
             dma((seqs, blocks)),
             dma((seqs, blocks)),

time: 153 us -> 133 us (0.87)
  local copies, waits for them, and re-layouts: 19.4 us -> 2.26 us
  Pallas kernels: 134 us -> 131 us
    unnamed x2 -> x1, local copies, waits for them, and re-layouts: 19.4 us -> 2.26 us
    pallas_call x1, Pallas kernels: 134 us -> 131 us  [fused(): pl.pallas_call(functools.partial(kernel, n_pipe, n_tensor), out_shape=jax...]
where the time goes in v2:
time: 133 us
  Pallas kernels  131 us (98%)
  local copies, waits for them, and re-layouts  2.26 us (2%)
    pallas_call x1, Pallas kernels, fused(): pl.pallas_call(functools.partial(kernel, n_pipe, n_tensor), out_shape=jax...  131 us

profile of v2, /device:TPU:8, one launch (start us, length us, event | category | flops | bytes accessed | tf_op | source)
XLA Modules:
  0.0 133.0 jit_solution(17757589553315950088)
XLA Ops:
  0.0 130.7 %shard_map.64 = bf16[2,256,1024]{2,1,0:T(8,128)(2,1)} custom-call(bf16[2,64,1024]{2,1,0:T(8,128)(2,1)} %mem_hbm.1, bf16[2,256,1024]{2,1,0:T(8,128)(2,1)} %bitcast.13, f32[1,4096]{1,0:T(1,128)} %gain_ref.1, bf16[4096,1024]{1,0:T(8,128)(2,1)} %bitcast.10, bf16[65536,128]{1,0:T(8,128)(2,1)} %bitcast.9, bf16[1024,4096]{1,0:T(8,128)(2,1)} %bitcast.11), custom_call_target="tpu_custom_call" | custom-call | tf_op jit(solution)/shard_map/pallas_call | solution.py:402
  130.7 2.3 %copy.9 = bf16[1,2,256,1024]{3,2,1,0:T(8,128)(2,1)} copy(bf16[1,2,256,1024]{3,2,1,0:T(8,128)(2,1)} %bitcast.12) | data formatting | bytes 2097152
